TPU v7x, 32 devices: a whole 2x2x4 slice. The times are simulated.
32 devices in a mesh: gx: 8 (over z, x), gy: 4 (over y, core).
Axes of the slice: x: 2, y: 2, z: 4, core: 2. Of those that a mesh axis runs over, the one named last changes fastest.
Arguments:
- parcel_props: float32 [16, 131072], P(None, ('gx', 'gy')), may hold values from -6 to 6
- size_class: int32 [131072], P(('gx', 'gy')), may hold values from 0 to 7
- dest_owner: int32 [131072, 1], P(('gx', 'gy')), may hold values from 0 to 31; in each aligned block of 4096 rows (0 to 4095, 4096 to 8191, ...) at most 512 rows name the same one
- dest_local: int32 [131072], P(('gx', 'gy')), may hold values from 0 to 4095
- class_table: float32 [8, 16], replicated, may hold values from 0.5 to 2
- gas_density: float32 [256, 512], P('gx', 'gy'), may hold values from 0.5 to 2
- gas_rest: float32 [4, 256, 512], P(None, 'gx', 'gy'), may hold values from -6 to 6
Outputs:
- new_density: float32 [256, 512], P('gx', 'gy')
- new_rest: float32 [4, 256, 512], P(None, 'gx', 'gy')
Inputs may be any that keep to these rules, and one draw needn't show every extreme that they name: `dest_owner`: among the parcels of one device, no owner device is named by more than 512 of them, a bound that some block reaches.
All inputs are finite; a program needn't handle non-finite values.
Results may differ from a plain program's by a relative error of at most 0.00015.
Values sent between devices are 32-bit elements; how exact they have to be, the bound alone decides.
A program may use at most 64 MiB of HBM per device.

v0:
```python
import functools

import jax
import jax.numpy as jnp
from jax import lax
from jax.experimental import pallas as pl
from jax.experimental.pallas import tpu as pltpu
from jax.sharding import PartitionSpec as P

F32 = jnp.float32
BF16 = jnp.bfloat16
LANES = 128
ROWS = 8
NT = (((1,), (1,)), ((), ()))


def split(x):
    high = x.astype(BF16).astype(F32)
    return high, x - high


def iota(shape, dim):
    return lax.broadcasted_iota(jnp.int32, shape, dim)


def bucket_kernel(
    devices, capacity, props_ref, class_ref, owner_ref, cell_ref, table_ref, out_ref, hot, vals
):
    props_count, parcels = props_ref.shape
    classes = table_ref.shape[0]
    chunks = parcels // LANES

    row, col = (iota((LANES, 2 * LANES), 0), iota((LANES, 2 * LANES), 1))
    upper = jnp.where((col >= LANES) | (row < col), 1.0, 0.0).astype(BF16)
    ids = iota((devices, LANES), 0)
    ranks = iota((capacity, LANES), 0)

    def member(c):
        return owner_ref[:, c * LANES : (c + 1) * LANES] == ids

    carry = jnp.zeros((devices, LANES), F32)
    for c in range(chunks):
        mine = member(c)
        counted = jnp.dot(
            jnp.where(mine, 1.0, 0.0).astype(BF16), upper, preferred_element_type=F32
        )
        rank = jnp.sum(
            jnp.where(mine, counted[:, :LANES] + carry, 0.0), axis=0, keepdims=True
        ).astype(jnp.int32)
        carry = carry + counted[:, LANES:]
        hot[:, c * LANES : (c + 1) * LANES] = jnp.where(ranks == rank, 1.0, 0.0).astype(BF16)

    eye = jnp.where(
        iota((props_count, props_count), 0) == iota((props_count, props_count), 1), 1.0, 0.0
    ).astype(BF16)
    table = jnp.concatenate(split(table_ref[...]), axis=0).astype(BF16)
    turned = lax.dot_general(eye, table, NT, preferred_element_type=F32).astype(BF16)
    picks = jnp.where(class_ref[...] == iota((classes, parcels), 0), 1.0, 0.0)
    picks = jnp.concatenate([picks, picks], axis=0).astype(BF16)
    coef = jnp.dot(turned, picks, preferred_element_type=F32)
    props = props_ref[...]
    which = iota((props_count, parcels), 0)
    weights = jnp.where(which >= 5, coef, jnp.where(which == 4, 1.0, 0.0))
    heat = jnp.sum(weights * props, axis=0, keepdims=True)
    which = iota((ROWS, parcels), 0)
    mixed = jnp.where(which == 0, jnp.exp(0.5 * props[0:1]), props[0:ROWS])
    mixed = jnp.where(which == 5, heat, mixed)
    mixed = jnp.where(which == 6, class_ref[...].astype(F32), mixed)
    mixed = jnp.where(which == 7, cell_ref[...].astype(F32), mixed)
    vals[...] = jnp.concatenate(split(mixed), axis=0)

    def group(g, unused):
        sends = [
            jnp.where(owner_ref[...] == g * ROWS + i, vals[...], 0.0).astype(BF16)
            for i in range(ROWS)
        ]
        packed = lax.dot_general(
            jnp.concatenate(sends, axis=0), hot[...], NT, preferred_element_type=F32
        )
        for i in range(ROWS):
            first = 2 * ROWS * i
            out_ref[g * ROWS + i] = (
                packed[first : first + ROWS] + packed[first + ROWS : first + 2 * ROWS]
            )
        return unused

    lax.fori_loop(0, devices // ROWS, group, 0)


def deposit_kernel(devices, capacity, got_ref, table_ref, dens_ref, rest_ref, out_ref, spot, gas, src, total):
    slab_x, slab_y = dens_ref.shape
    classes = table_ref.shape[0]
    fields = jnp.concatenate([dens_ref[...], rest_ref[...].reshape(4 * slab_x, slab_y)], axis=0)
    tab = jnp.concatenate(split(fields), axis=1).astype(BF16)
    total[...] = jnp.zeros_like(total)
    ys = iota((slab_y, capacity), 0)
    xs = iota((slab_x, capacity), 0)

    def group(g, unused):
        def cell_of(i):
            return got_ref[(g * ROWS + i)][7:8].astype(jnp.int32)

        def part(c):
            return jnp.concatenate([got_ref[g * ROWS + i][c : c + 1] for i in range(ROWS)], axis=0)

        for i in range(ROWS):
            cell = cell_of(i)
            hot = jnp.where(ys == cell % slab_y, 1.0, 0.0).astype(BF16)
            spot[:, i * capacity : (i + 1) * capacity] = hot
            found = jnp.dot(tab, jnp.concatenate([hot, hot], axis=0), preferred_element_type=F32)
            in_row = xs == cell // slab_y
            for c in range(5):
                gas[c, i : i + 1] = jnp.sum(
                    jnp.where(in_row, found[c * slab_x : (c + 1) * slab_x], 0.0),
                    axis=0,
                    keepdims=True,
                )

        kind = part(6).astype(jnp.int32)
        coef = [jnp.full(kind.shape, table_ref[0, j], F32) for j in range(5)]
        for k in range(1, classes):
            same = kind == k
            coef = [jnp.where(same, table_ref[k, j], coef[j]) for j in range(5)]
        mass = part(0)
        speed = [part(j) for j in (1, 2, 3)]
        heat, energy = part(4), part(5)
        inverse = 1.0 / gas[0]
        slip = [speed[j] - gas[j + 1] * inverse for j in range(3)]
        excess = heat - gas[4] * inverse
        soft = jnp.maximum(excess, 0.0) + jnp.log1p(jnp.exp(-jnp.abs(excess)))
        evapor = mass * (1.0 - jnp.exp(-(coef[0] * soft)))
        square = slip[0] * slip[0] + slip[1] * slip[1] + slip[2] * slip[2]
        drag = mass * (1.0 - jnp.exp(-coef[1] * jnp.sqrt(1.0 + square)))
        out = [evapor]
        out += [evapor * coef[2 + j] * speed[j] + drag * slip[j] for j in range(3)]
        out += [evapor * energy]
        for c in range(5):
            high, low = split(out[c])
            src[c] = high
            src[5 + c] = low

        for i in range(ROWS):
            in_row = xs == cell_of(i) // slab_y
            spread = [jnp.where(in_row, src[c, i : i + 1], 0.0).astype(BF16) for c in range(10)]
            total[...] += lax.dot_general(
                jnp.concatenate(spread, axis=0),
                spot[:, i * capacity : (i + 1) * capacity],
                NT,
                preferred_element_type=F32,
            )
        return unused

    lax.fori_loop(0, devices // ROWS, group, 0)
    half = 5 * slab_x
    out_ref[...] = (total[:half] + total[half:]).reshape(5, slab_x, slab_y)


def with_halo(deposit):
    pieces = []
    for axis, dim in (("gx", 1), ("gy", 2)):
        devices, length = (lax.axis_size(axis), deposit.shape[dim])
        up = [(i, i + 1) for i in range(devices - 1)]
        down = [(j, i) for i, j in up]
        last = lax.slice_in_dim(deposit, length - 1, length, axis=dim)
        leading = lax.slice_in_dim(deposit, 0, 1, axis=dim)
        before = lax.ppermute(last, axis, up)
        after = lax.ppermute(leading, axis, down)
        pieces.append(
            jnp.concatenate([before, lax.slice_in_dim(deposit, 0, length - 1, axis=dim)], axis=dim)
            + jnp.concatenate([lax.slice_in_dim(deposit, 1, length, axis=dim), after], axis=dim)
        )
    return pieces[0] + pieces[1]


def per_device(
    parcel_props, size_class, dest_owner, dest_local, class_table, gas_density, gas_rest
):
    devices = lax.axis_size("gx") * lax.axis_size("gy")
    props_count, parcels = parcel_props.shape
    slab_x, slab_y = gas_density.shape
    capacity = -(-max(2, 4 * parcels // devices) // LANES) * LANES
    vmem = pl.BlockSpec(memory_space=pltpu.VMEM)
    smem = pl.BlockSpec(memory_space=pltpu.SMEM)
    packed = pl.pallas_call(
        functools.partial(bucket_kernel, devices, capacity),
        out_shape=jax.ShapeDtypeStruct((devices, ROWS, capacity), F32),
        in_specs=[vmem] * 5,
        out_specs=vmem,
        scratch_shapes=[
            pltpu.VMEM((capacity, parcels), BF16),
            pltpu.VMEM((2 * ROWS, parcels), F32),
        ],
    )(
        parcel_props,
        size_class.reshape(1, parcels),
        dest_owner.reshape(1, parcels),
        dest_local.reshape(1, parcels),
        class_table,
    )
    got = lax.all_to_all(packed, ("gx", "gy"), split_axis=0, concat_axis=0, tiled=True)
    deposit = pl.pallas_call(
        functools.partial(deposit_kernel, devices, capacity),
        out_shape=jax.ShapeDtypeStruct((5, slab_x, slab_y), F32),
        in_specs=[vmem, smem, vmem, vmem],
        out_specs=vmem,
        scratch_shapes=[
            pltpu.VMEM((slab_y, ROWS * capacity), BF16),
            pltpu.VMEM((5, ROWS, capacity), F32),
            pltpu.VMEM((10, ROWS, capacity), F32),
            pltpu.VMEM((10 * slab_x, slab_y), F32),
        ],
    )(got, class_table, gas_density, gas_rest)
    smooth = 0.4 * deposit + 0.15 * with_halo(deposit)
    return (gas_density + smooth[0], gas_rest + smooth[1:])


def solution(mesh):
    return jax.shard_map(
        per_device,
        mesh=mesh,
        in_specs=(
            P(None, ("gx", "gy")),
            P(("gx", "gy")),
            P(("gx", "gy"), None),
            P(("gx", "gy")),
            P(),
            P("gx", "gy"),
            P(None, "gx", "gy"),
        ),
        out_specs=(P("gx", "gy"), P(None, "gx", "gy")),
        check_vma=False,
    )
```

profile of v0, /device:TPU:1, one launch (start us, length us, event | category | flops | bytes accessed | tf_op | source)
XLA Modules:
  0.0 58.9 jit_solution(14966990687622767901)
XLA Ops:
  0.6 10.5 %shard_map.86 = f32[32,8,512]{2,1,0:T(8,128)} custom-call(f32[16,4096]{1,0:T(8,128)} %props_ref.1, s32[1,4096]{1,0:T(1,128)} %bitcast.7, s32[1,4096]{1,0:T(1,128)} %bitcast.8, s32[1,4096]{1,0:T(1,128)} %bitcast.9, f32[8,16]{1,0:T(8,128)} %table_ref.3), custom_call_target="tpu_custom_call" | custom-call | tf_op jit(solution)/shard_map/pallas_call | solution.py:184
  11.2 22.4 %all_to_all.5.got_ref = f32[32,8,512]{2,1,0:T(8,128)} all-to-all(f32[32,8,512]{2,1,0:T(8,128)} %shard_map.86), channel_id=1, replica_groups=mesh['gx'=8,'gy'=4] {'gx','gy'}, dimensions={0} | all-to-all | bytes 1048576 | tf_op jit(solution)/shard_map/all_to_all | solution.py:200
  33.6 9.1 %shard_map.87 = f32[5,32,128]{2,1,0:T(8,128)} custom-call(f32[32,8,512]{2,1,0:T(8,128)} %all_to_all.5.got_ref, f32[8,16]{1,0:T(8,128)} %table_ref.3, f32[32,128]{1,0:T(8,128)} %dens_ref.1, f32[4,32,128]{2,1,0:T(8,128)} %rest_ref.1), custom_call_target="tpu_custom_call" | custom-call | tf_op jit(solution)/shard_map/pallas_call | solution.py:201
  42.7 0.7 %fusion.7 = (f32[5,1,128]{2,1,0:T(1,128)S(1)}, f32[5,1,128]{2,1,0:T(1,128)S(1)}) fusion(f32[5,32,128]{2,1,0:T(8,128)} %shard_map.87), kind=kLoop, calls=%fused_computation.11 | loop fusion | bytes 10240 | tf_op jit(solution)/shard_map/slice | solution.py:165
  43.4 0.0 copy-start
  43.4 1.0 %fusion.6 = (f32[5,31,128]{2,1,0:T(8,128)S(1)}, f32[5,31,128]{2,1,0:T(8,128)S(1)}) fusion(f32[5,32,128]{2,1,0:T(8,128)} %shard_map.87), kind=kLoop, calls=%fused_computation.10 | loop fusion | bytes 317440 | tf_op jit(solution)/shard_map/slice | solution.py:170
  44.5 0.0 copy-done
  44.5 0.1 fusion.5
  44.6 1.3 %collective-permute-start.1 = (f32[5,1,128]{2,1,0:T(1,128)S(1)}, f32[5,1,128]{2,1,0:T(1,128)S(1)}, u32[]{:S(2)}, u32[]{:S(2)}) collective-permute-start(f32[5,1,128]{2,1,0:T(1,128)S(1)} %get-tuple-element.8), channel_id=1, source_target_pairs={{4,0},{8,4},{12,8},{16,12},{20,16},{24,20},{28,24},{5,1},{9,5},{13... | collective-permute-start | bytes 7688 | tf_op jit(solution)/shard_map/ppermute | solution.py:167
  45.9 4.0 %collective-permute-start = (f32[5,1,128]{2,1,0:T(1,128)S(1)}, f32[5,1,128]{2,1,0:T(1,128)S(1)}, u32[]{:S(2)}, u32[]{:S(2)}) collective-permute-start(f32[5,1,128]{2,1,0:T(1,128)S(1)} %get-tuple-element.9), channel_id=1, source_target_pairs={{0,4},{4,8},{8,12},{12,16},{16,20},{20,24},{24,28},{1,5},{5,9},{9,... | collective-permute-start | bytes 7688 | tf_op jit(solution)/shard_map/ppermute | solution.py:166
  49.9 3.1 %collective-permute-start.3 = (f32[5,32,1]{2,1,0:T(8,128)S(1)}, f32[5,32,1]{2,1,0:T(8,128)S(1)}, u32[]{:S(2)}, u32[]{:S(2)}) collective-permute-start(f32[5,32,1]{2,1,0:T(8,128)S(1)} %get-tuple-element.4), channel_id=1, source_target_pairs={{1,0},{2,1},{3,2},{5,4},{6,5},{7,6},{9,8},{10,9},{11,10},{13,12},{... | collective-permute-start | bytes 1928 | tf_op jit(solution)/shard_map/ppermute | solution.py:167
  53.0 2.4 %collective-permute-start.2 = (f32[5,32,1]{2,1,0:T(8,128)S(1)}, f32[5,32,1]{2,1,0:T(8,128)S(1)}, u32[]{:S(2)}, u32[]{:S(2)}) collective-permute-start(f32[5,32,1]{2,1,0:T(8,128)S(1)} %get-tuple-element.5), channel_id=1, source_target_pairs={{0,1},{1,2},{2,3},{4,5},{5,6},{6,7},{8,9},{9,10},{10,11},{12,13},{... | collective-permute-start | bytes 1928 | tf_op jit(solution)/shard_map/ppermute | solution.py:166
  55.5 0.1 fusion.4
  55.6 0.1 collective-permute-done.3
  55.6 1.3 %collective-permute-done.2 = f32[5,32,1]{2,1,0:T(8,128)S(1)} collective-permute-done((f32[5,32,1]{2,1,0:T(8,128)S(1)}, f32[5,32,1]{2,1,0:T(8,128)S(1)}, u32[]{:S(2)}, u32[]{:S(2)}) %collective-permute-start.2) | collective-permute-done | bytes 672 | tf_op jit(solution)/shard_map/ppermute | solution.py:166
  56.9 0.0 collective-permute-done.1
  56.9 0.0 collective-permute-done
  56.9 0.0 copy-start.2
  56.9 0.0 copy-start.1
  56.9 0.1 fusion.2
  57.1 0.6 copy-done.2
  57.7 0.6 %fusion.3 = f32[32,128]{1,0:T(8,128)} fusion(f32[32,128]{1,0:T(8,128)S(1)} %copy-done.2, f32[5,32,128]{2,1,0:T(8,128)S(1)} %fusion.2), kind=kLoop, calls=%fused_computation.7 | loop fusion | flops 4096 | bytes 49152 | tf_op jit(solution)/shard_map/add | solution.py:214
  58.3 0.0 copy-done.1
  58.3 0.6 %slice_add_fusion = f32[4,32,128]{2,1,0:T(8,128)} fusion(f32[4,32,128]{2,1,0:T(8,128)S(1)} %copy-done.1, f32[5,32,128]{2,1,0:T(8,128)S(1)} %fusion.2), kind=kLoop, calls=%fused_computation.5 | loop fusion | flops 16384 | bytes 196608 | tf_op jit(solution)/shard_map/add | solution.py:214
Async XLA Ops:
  43.4 1.1 %copy-start = (f32[5,32,128]{2,1,0:T(8,128)S(1)}, f32[5,32,128]{2,1,0:T(8,128)}, u32[]{:S(2)}) copy-start(f32[5,32,128]{2,1,0:T(8,128)} %shard_map.87) | copy-start | bytes 245764
  44.6 12.3 %collective-permute-start.1 = (f32[5,1,128]{2,1,0:T(1,128)S(1)}, f32[5,1,128]{2,1,0:T(1,128)S(1)}, u32[]{:S(2)}, u32[]{:S(2)}) collective-permute-start(f32[5,1,128]{2,1,0:T(1,128)S(1)} %get-tuple-element.8), channel_id=1, source_target_pairs={{4,0},{8,4},{12,8},{16,12},{20,16},{24,20},{28,24},{5,1},{9,5},{13... | collective-permute-start | bytes 7688 | tf_op jit(solution)/shard_map/ppermute | solution.py:167
  45.9 11.0 %collective-permute-start = (f32[5,1,128]{2,1,0:T(1,128)S(1)}, f32[5,1,128]{2,1,0:T(1,128)S(1)}, u32[]{:S(2)}, u32[]{:S(2)}) collective-permute-start(f32[5,1,128]{2,1,0:T(1,128)S(1)} %get-tuple-element.9), channel_id=1, source_target_pairs={{0,4},{4,8},{8,12},{12,16},{16,20},{20,24},{24,28},{1,5},{5,9},{9,... | collective-permute-start | bytes 7688 | tf_op jit(solution)/shard_map/ppermute | solution.py:166
  49.9 5.8 %collective-permute-start.3 = (f32[5,32,1]{2,1,0:T(8,128)S(1)}, f32[5,32,1]{2,1,0:T(8,128)S(1)}, u32[]{:S(2)}, u32[]{:S(2)}) collective-permute-start(f32[5,32,1]{2,1,0:T(8,128)S(1)} %get-tuple-element.4), channel_id=1, source_target_pairs={{1,0},{2,1},{3,2},{5,4},{6,5},{7,6},{9,8},{10,9},{11,10},{13,12},{... | collective-permute-start | bytes 1928 | tf_op jit(solution)/shard_map/ppermute | solution.py:167
  53.0 3.9 %collective-permute-start.2 = (f32[5,32,1]{2,1,0:T(8,128)S(1)}, f32[5,32,1]{2,1,0:T(8,128)S(1)}, u32[]{:S(2)}, u32[]{:S(2)}) collective-permute-start(f32[5,32,1]{2,1,0:T(8,128)S(1)} %get-tuple-element.5), channel_id=1, source_target_pairs={{0,1},{1,2},{2,3},{4,5},{5,6},{6,7},{8,9},{9,10},{10,11},{12,13},{... | collective-permute-start | bytes 1928 | tf_op jit(solution)/shard_map/ppermute | solution.py:166
  56.9 0.7 %copy-start.2 = (f32[32,128]{1,0:T(8,128)S(1)}, f32[32,128]{1,0:T(8,128)}, u32[]{:S(2)}) copy-start(f32[32,128]{1,0:T(8,128)} %dens_ref.1) | copy-start | bytes 49156
  56.9 1.3 %copy-start.1 = (f32[4,32,128]{2,1,0:T(8,128)S(1)}, f32[4,32,128]{2,1,0:T(8,128)}, u32[]{:S(2)}) copy-start(f32[4,32,128]{2,1,0:T(8,128)} %rest_ref.1) | copy-start | bytes 196612
where the time goes:
time: 59.9 us; the launch traced here: 58.9 us
  blocking collectives  22.4 us (37%)
  Pallas kernels  19.7 us (33%)
  starting transfers between devices  10.8 us (18%)
  local copies, waits for them, and re-layouts  2.56 us (4%)
  waiting for transfers between devices  1.38 us (2%)
  other arithmetic  1.37 us (2%)
  between operations  0.7 us (1%)
    all_to_all x1, blocking collectives, per_device(): lax.all_to_all(packed, ('gx', 'gy'), split_axis=0, concat_axis=0, tiled=T...  22.4 us
    pallas_call x1, Pallas kernels, per_device(): pl.pallas_call(functools.partial(bucket_kernel, devices, capacity), out_s...  10.5 us
    pallas_call x1, Pallas kernels, per_device(): pl.pallas_call(functools.partial(deposit_kernel, devices, capacity), out_...  9.12 us
    ppermute x2, starting transfers between devices, with_halo(): before = lax.ppermute(last, axis, up)  6.41 us
    ppermute x2, starting transfers between devices, with_halo(): after = lax.ppermute(leading, axis, down)  4.43 us
    ppermute x2, waiting for transfers between devices, with_halo(): before = lax.ppermute(last, axis, up)  1.28 us
    add x2, other arithmetic, per_device(): return (gas_density + smooth[0], gas_rest + smooth[1:])  1.25 us
  transfers between devices with their start and end apart: 4, of which 2 were waited for; matrix products, arithmetic and copies ran while one was open for 0% of the time, Pallas kernels for 0%

commit v1 on v0

v1 whole, which is shorter than its diff:
```python
import functools

import jax
import jax.numpy as jnp
from jax import lax
from jax.experimental import pallas as pl
from jax.experimental.pallas import tpu as pltpu
from jax.sharding import PartitionSpec as P

F32 = jnp.float32
BF16 = jnp.bfloat16
LANES = 128
ROWS = 8
NT = (((1,), (1,)), ((), ()))


def split(x):
    high = x.astype(BF16).astype(F32)
    return high, x - high


def iota(shape, dim):
    return lax.broadcasted_iota(jnp.int32, shape, dim)


def fused_kernel(
    width_x,
    width_y,
    capacity,
    props_ref,
    class_ref,
    owner_ref,
    cell_ref,
    table_ref,
    scalars_ref,
    dens_ref,
    rest_ref,
    new_dens_ref,
    new_rest_ref,
    hot,
    vals,
    packed,
    got,
    spot,
    gas,
    src,
    total,
    row_out,
    row_in,
    col_out,
    col_in,
    send_sem,
    recv_sem,
    halo_send,
    halo_recv,
):
    devices = width_x * width_y
    groups = devices // ROWS
    my_x, my_y = lax.axis_index("gx"), lax.axis_index("gy")
    me = my_x * width_y + my_y
    props_count, parcels = props_ref.shape
    classes = table_ref.shape[0]
    slab_x, slab_y = dens_ref.shape

    def place(device):
        return (device // width_y, device % width_y)

    barrier = pltpu.get_barrier_semaphore()

    def greet(k, unused):
        pl.semaphore_signal(
            barrier,
            inc=1,
            device_id=place((me + k) % devices),
            device_id_type=pl.DeviceIdType.MESH,
        )
        return unused

    lax.fori_loop(1, devices, greet, 0)

    def group_at(step):
        turn = (1 - 2 * (step % 2)) * ((step + 1) // 2)
        return (me // ROWS + groups // 2 + turn + groups) % groups

    def copy_to(device):
        return pltpu.make_async_remote_copy(
            src_ref=packed.at[device],
            dst_ref=got.at[me],
            send_sem=send_sem.at[device],
            recv_sem=recv_sem.at[me],
            device_id=place(device),
            device_id_type=pl.DeviceIdType.MESH,
        )

    def copy_from(device):
        return pltpu.make_async_remote_copy(
            src_ref=packed.at[device],
            dst_ref=got.at[device],
            send_sem=send_sem.at[device],
            recv_sem=recv_sem.at[device],
            device_id=place(device),
            device_id_type=pl.DeviceIdType.MESH,
        )

    row, col = (iota((LANES, 2 * LANES), 0), iota((LANES, 2 * LANES), 1))
    upper = jnp.where((col >= LANES) | (row < col), 1.0, 0.0).astype(BF16)
    ids = iota((devices, LANES), 0)
    ranks = iota((capacity, LANES), 0)
    carry = jnp.zeros((devices, LANES), F32)
    for c in range(parcels // LANES):
        mine = owner_ref[:, c * LANES : (c + 1) * LANES] == ids
        counted = jnp.dot(
            jnp.where(mine, 1.0, 0.0).astype(BF16), upper, preferred_element_type=F32
        )
        rank = jnp.sum(
            jnp.where(mine, counted[:, :LANES] + carry, 0.0), axis=0, keepdims=True
        ).astype(jnp.int32)
        carry = carry + counted[:, LANES:]
        hot[:, c * LANES : (c + 1) * LANES] = jnp.where(ranks == rank, 1.0, 0.0).astype(BF16)

    eye = jnp.where(
        iota((props_count, props_count), 0) == iota((props_count, props_count), 1), 1.0, 0.0
    ).astype(BF16)
    table = jnp.concatenate(split(table_ref[...]), axis=0).astype(BF16)
    turned = lax.dot_general(eye, table, NT, preferred_element_type=F32).astype(BF16)
    picks = jnp.where(class_ref[...] == iota((classes, parcels), 0), 1.0, 0.0)
    picks = jnp.concatenate([picks, picks], axis=0).astype(BF16)
    coef = jnp.dot(turned, picks, preferred_element_type=F32)
    props = props_ref[...]
    which = iota((props_count, parcels), 0)
    weights = jnp.where(which >= 5, coef, jnp.where(which == 4, 1.0, 0.0))
    heat_sum = jnp.sum(weights * props, axis=0, keepdims=True)
    which = iota((ROWS, parcels), 0)
    mixed = jnp.where(which == 0, jnp.exp(0.5 * props[0:1]), props[0:ROWS])
    mixed = jnp.where(which == 5, heat_sum, mixed)
    mixed = jnp.where(which == 6, class_ref[...].astype(F32), mixed)
    mixed = jnp.where(which == 7, cell_ref[...].astype(F32), mixed)
    vals[...] = jnp.concatenate(split(mixed), axis=0)

    pl.semaphore_wait(barrier, devices - 1)

    def send_group(step, unused):
        first = group_at(step) * ROWS
        sends = [
            jnp.where(owner_ref[...] == first + i, vals[...], 0.0).astype(BF16)
            for i in range(ROWS)
        ]
        both = lax.dot_general(
            jnp.concatenate(sends, axis=0), hot[...], NT, preferred_element_type=F32
        )
        for i in range(ROWS):
            at = 2 * ROWS * i
            packed[first + i] = both[at : at + ROWS] + both[at + ROWS : at + 2 * ROWS]

        def launch(i, carried):
            device = first + i

            @pl.when(device != me)
            def _():
                copy_to(device).start()

            return carried

        return lax.fori_loop(0, ROWS, launch, unused)

    lax.fori_loop(0, groups, send_group, 0)
    got[me] = packed[me]

    fields = jnp.concatenate([dens_ref[...], rest_ref[...].reshape(4 * slab_x, slab_y)], axis=0)
    tab = jnp.concatenate(split(fields), axis=1).astype(BF16)
    total[...] = jnp.zeros_like(total)
    ys = iota((slab_y, capacity), 0)
    xs = iota((slab_x, capacity), 0)

    def take_group(step, unused):
        first = group_at(step) * ROWS

        def arrive(i, carried):
            @pl.when(first + i != me)
            def _():
                copy_from(first + i).wait_recv()

            return carried

        lax.fori_loop(0, ROWS, arrive, 0)

        def cell_of(i):
            return got[first + i][7:8].astype(jnp.int32)

        def part(c):
            return jnp.concatenate([got[first + i][c : c + 1] for i in range(ROWS)], axis=0)

        for i in range(ROWS):
            cell = cell_of(i)
            lane_hot = jnp.where(ys == cell % slab_y, 1.0, 0.0).astype(BF16)
            spot[:, i * capacity : (i + 1) * capacity] = lane_hot
            found = jnp.dot(
                tab, jnp.concatenate([lane_hot, lane_hot], axis=0), preferred_element_type=F32
            )
            in_row = xs == cell // slab_y
            for c in range(5):
                gas[c, i : i + 1] = jnp.sum(
                    jnp.where(in_row, found[c * slab_x : (c + 1) * slab_x], 0.0),
                    axis=0,
                    keepdims=True,
                )

        kind = part(6).astype(jnp.int32)
        coefs = [jnp.full(kind.shape, scalars_ref[0, j], F32) for j in range(5)]
        for k in range(1, classes):
            same = kind == k
            coefs = [jnp.where(same, scalars_ref[k, j], coefs[j]) for j in range(5)]
        mass = part(0)
        speed = [part(j) for j in (1, 2, 3)]
        heat, energy = part(4), part(5)
        inverse = 1.0 / gas[0]
        slip = [speed[j] - gas[j + 1] * inverse for j in range(3)]
        excess = heat - gas[4] * inverse
        soft = jnp.maximum(excess, 0.0) + jnp.log1p(jnp.exp(-jnp.abs(excess)))
        evapor = mass * (1.0 - jnp.exp(-(coefs[0] * soft)))
        square = slip[0] * slip[0] + slip[1] * slip[1] + slip[2] * slip[2]
        drag = mass * (1.0 - jnp.exp(-coefs[1] * jnp.sqrt(1.0 + square)))
        out = [evapor]
        out += [evapor * coefs[2 + j] * speed[j] + drag * slip[j] for j in range(3)]
        out += [evapor * energy]
        for c in range(5):
            high, low = split(out[c])
            src[c] = high
            src[5 + c] = low

        for i in range(ROWS):
            in_row = xs == cell_of(i) // slab_y
            spread = [jnp.where(in_row, src[c, i : i + 1], 0.0).astype(BF16) for c in range(10)]
            total[...] += lax.dot_general(
                jnp.concatenate(spread, axis=0),
                spot[:, i * capacity : (i + 1) * capacity],
                NT,
                preferred_element_type=F32,
            )
        return unused

    lax.fori_loop(0, groups, take_group, 0)

    half = 5 * slab_x
    deposit = [
        total[c * slab_x : (c + 1) * slab_x]
        + total[half + c * slab_x : half + (c + 1) * slab_x]
        for c in range(5)
    ]
    lane = iota((slab_x, slab_y), 1)
    low_edge = jnp.zeros((slab_x, slab_y), F32)
    high_edge = jnp.zeros((slab_x, slab_y), F32)
    row_out[...] = jnp.zeros_like(row_out)
    for c in range(5):
        row_out[0, c : c + 1] = deposit[c][0:1]
        row_out[1, c : c + 1] = deposit[c][slab_x - 1 : slab_x]
        low_edge = jnp.where(
            lane == c, pltpu.roll(deposit[c], c, 1) if c else deposit[c], low_edge
        )
        high_edge = jnp.where(lane == c, pltpu.roll(deposit[c], c + 1, 1), high_edge)
    col_out[0] = low_edge
    col_out[1] = high_edge

    def edge(out_ref, in_ref, side, base, target):
        return pltpu.make_async_remote_copy(
            src_ref=out_ref.at[side],
            dst_ref=in_ref.at[side],
            send_sem=halo_send.at[base + side],
            recv_sem=halo_recv.at[base + side],
            device_id=target,
            device_id_type=pl.DeviceIdType.MESH,
        )

    edges = [
        (row_out, row_in, 0, 0, (my_x - 1, my_y), my_x > 0, my_x < width_x - 1),
        (row_out, row_in, 1, 0, (my_x + 1, my_y), my_x < width_x - 1, my_x > 0),
        (col_out, col_in, 0, 2, (my_x, my_y - 1), my_y > 0, my_y < width_y - 1),
        (col_out, col_in, 1, 2, (my_x, my_y + 1), my_y < width_y - 1, my_y > 0),
    ]
    for out_ref, in_ref, side, base, target, sends, takes in edges:

        @pl.when(sends)
        def _(out_ref=out_ref, in_ref=in_ref, side=side, base=base, target=target):
            edge(out_ref, in_ref, side, base, target).start()

        @pl.when(jnp.logical_not(takes))
        def _(in_ref=in_ref, side=side):
            in_ref[side] = jnp.zeros(in_ref.shape[1:], F32)

    def wait_sent(k, unused):
        copy_to((me + k) % devices).wait_send()
        return unused

    lax.fori_loop(1, devices, wait_sent, 0)
    for out_ref, in_ref, side, base, target, sends, takes in edges:

        @pl.when(takes)
        def _(out_ref=out_ref, in_ref=in_ref, side=side, base=base, target=target):
            edge(out_ref, in_ref, side, base, target).wait_recv()

    for c in range(5):
        here = deposit[c]
        above = jnp.concatenate([row_in[1, c : c + 1], here[: slab_x - 1]], axis=0)
        below = jnp.concatenate([here[1:], row_in[0, c : c + 1]], axis=0)
        left_in = pltpu.roll(col_in[1], slab_y - c, 1) if c else col_in[1]
        left = jnp.where(lane == 0, left_in, pltpu.roll(here, 1, 1))
        right = jnp.where(
            lane == slab_y - 1,
            pltpu.roll(col_in[0], slab_y - 1 - c, 1),
            pltpu.roll(here, slab_y - 1, 1),
        )
        smooth = 0.4 * here + 0.15 * (below + above + right + left)
        if c == 0:
            new_dens_ref[...] = dens_ref[...] + smooth
        else:
            new_rest_ref[c - 1] = rest_ref[c - 1] + smooth

    for out_ref, in_ref, side, base, target, sends, takes in edges:

        @pl.when(sends)
        def _(out_ref=out_ref, in_ref=in_ref, side=side, base=base, target=target):
            edge(out_ref, in_ref, side, base, target).wait_send()


def per_device(
    parcel_props, size_class, dest_owner, dest_local, class_table, gas_density, gas_rest
):
    width_x, width_y = lax.axis_size("gx"), lax.axis_size("gy")
    devices = width_x * width_y
    props_count, parcels = parcel_props.shape
    slab_x, slab_y = gas_density.shape
    capacity = -(-max(2, 4 * parcels // devices) // LANES) * LANES
    vmem = pl.BlockSpec(memory_space=pltpu.VMEM)
    smem = pl.BlockSpec(memory_space=pltpu.SMEM)
    return pl.pallas_call(
        functools.partial(fused_kernel, width_x, width_y, capacity),
        out_shape=(
            jax.ShapeDtypeStruct(gas_density.shape, F32),
            jax.ShapeDtypeStruct(gas_rest.shape, F32),
        ),
        in_specs=[vmem] * 5 + [smem] + [vmem] * 2,
        out_specs=(vmem, vmem),
        scratch_shapes=[
            pltpu.VMEM((capacity, parcels), BF16),
            pltpu.VMEM((2 * ROWS, parcels), F32),
            pltpu.VMEM((devices, ROWS, capacity), F32),
            pltpu.VMEM((devices, ROWS, capacity), F32),
            pltpu.VMEM((slab_y, ROWS * capacity), BF16),
            pltpu.VMEM((5, ROWS, capacity), F32),
            pltpu.VMEM((10, ROWS, capacity), F32),
            pltpu.VMEM((10 * slab_x, slab_y), F32),
            pltpu.VMEM((2, ROWS, slab_y), F32),
            pltpu.VMEM((2, ROWS, slab_y), F32),
            pltpu.VMEM((2, slab_x, slab_y), F32),
            pltpu.VMEM((2, slab_x, slab_y), F32),
            pltpu.SemaphoreType.DMA((devices,)),
            pltpu.SemaphoreType.DMA((devices,)),
            pltpu.SemaphoreType.DMA((4,)),
            pltpu.SemaphoreType.DMA((4,)),
        ],
        compiler_params=pltpu.CompilerParams(collective_id=0, has_side_effects=True),
    )(
        parcel_props,
        size_class.reshape(1, parcels),
        dest_owner.reshape(1, parcels),
        dest_local.reshape(1, parcels),
        class_table,
        class_table,
        gas_density,
        gas_rest,
    )


def solution(mesh):
    return jax.shard_map(
        per_device,
        mesh=mesh,
        in_specs=(
            P(None, ("gx", "gy")),
            P(("gx", "gy")),
            P(("gx", "gy"), None),
            P(("gx", "gy")),
            P(),
            P("gx", "gy"),
            P(None, "gx", "gy"),
        ),
        out_specs=(P("gx", "gy"), P(None, "gx", "gy")),
        check_vma=False,
    )
```

time: 59.9 us -> 36 us (0.60)
  the two profiles are of different devices: /device:TPU:1 before, /device:TPU:0 now
where the time goes in v1:
time: 36 us; the launch traced here: 35.7 us
  Pallas kernels  32.3 us (90%)
  local copies, waits for them, and re-layouts  2.8 us (8%)
  between operations  0.64 us (2%)
    pallas_call x1, Pallas kernels, per_device(): pl.pallas_call(functools.partial(fused_kernel, width_x, width_y, capacity...  32.3 us
    unnamed x2, local copies, waits for them, and re-layouts  2.8 us

profile of v1, /device:TPU:0, one launch (start us, length us, event | category | flops | bytes accessed | tf_op | source)
XLA Modules:
  0.0 35.7 jit_solution(682992483081496706)
XLA Ops:
  0.6 32.3 %shard_map.86 = (f32[32,128]{1,0:T(8,128)}, f32[4,32,128]{2,1,0:T(8,128)}) custom-call(f32[16,4096]{1,0:T(8,128)} %props_ref.1, s32[1,4096]{1,0:T(1,128)} %bitcast.3, s32[1,4096]{1,0:T(1,128)} %bitcast.4, s32[1,4096]{1,0:T(1,128)} %bitcast.5, f32[8,16]{1,0:T(8,128)} %scalars_ref.1, f32[8,16]{1,0:T(8,128)} %scalars_ref.1, f32[32,128]{1,0:T(8,128)} %dens_ref.1, ...), custom_call_target="tpu_custom_call" | custom-call | tf_op jit(solution)/shard_map/pallas_call | solution.py:335
  32.9 1.3 %copy.11 = f32[32,128]{1,0:T(8,128)} copy(f32[32,128]{1,0:T(8,128)} %get-tuple-element.4) | data formatting | bytes 32768
  34.2 1.5 %copy.12 = f32[4,32,128]{2,1,0:T(8,128)} copy(f32[4,32,128]{2,1,0:T(8,128)} %get-tuple-element.5) | data formatting | bytes 131072

commit v2 on v1

--- a/solution.py
+++ b/solution.py
@@ -11,6 +11,7 @@
 BF16 = jnp.bfloat16
 LANES = 128
 ROWS = 8
+BATCH = 16
 NT = (((1,), (1,)), ((), ()))
 
 
@@ -35,10 +36,10 @@
     scalars_ref,
     dens_ref,
     rest_ref,
-    new_dens_ref,
-    new_rest_ref,
+    smooth_ref,
     hot,
     vals,
+    owners,
     packed,
     got,
     spot,
@@ -56,6 +57,7 @@
 ):
     devices = width_x * width_y
     groups = devices // ROWS
+    batch = BATCH
     my_x, my_y = lax.axis_index("gx"), lax.axis_index("gy")
     me = my_x * width_y + my_y
     props_count, parcels = props_ref.shape
@@ -105,7 +107,9 @@
     row, col = (iota((LANES, 2 * LANES), 0), iota((LANES, 2 * LANES), 1))
     upper = jnp.where((col >= LANES) | (row < col), 1.0, 0.0).astype(BF16)
     ids = iota((devices, LANES), 0)
-    ranks = iota((capacity, LANES), 0)
+    wide = min(capacity, 256)
+    ranks = iota((wide, LANES), 0).astype(F32).astype(BF16)
+    one, zero = jnp.ones((), BF16), jnp.zeros((), BF16)
     carry = jnp.zeros((devices, LANES), F32)
     for c in range(parcels // LANES):
         mine = owner_ref[:, c * LANES : (c + 1) * LANES] == ids
@@ -114,9 +118,13 @@
         )
         rank = jnp.sum(
             jnp.where(mine, counted[:, :LANES] + carry, 0.0), axis=0, keepdims=True
-        ).astype(jnp.int32)
+        )
         carry = carry + counted[:, LANES:]
-        hot[:, c * LANES : (c + 1) * LANES] = jnp.where(ranks == rank, 1.0, 0.0).astype(BF16)
+        for start in range(0, capacity, wide):
+            local = jnp.clip(rank - start, -1.0, 256.0).astype(BF16)
+            hot[start : start + wide, c * LANES : (c + 1) * LANES] = jnp.where(
+                ranks == local, one, zero
+            )
 
     eye = jnp.where(
         iota((props_count, props_count), 0) == iota((props_count, props_count), 1), 1.0, 0.0
@@ -135,20 +143,25 @@
     mixed = jnp.where(which == 5, heat_sum, mixed)
     mixed = jnp.where(which == 6, class_ref[...].astype(F32), mixed)
     mixed = jnp.where(which == 7, cell_ref[...].astype(F32), mixed)
-    vals[...] = jnp.concatenate(split(mixed), axis=0)
+    vals[...] = jnp.concatenate(split(mixed), axis=0).astype(BF16)
+    owners[...] = jnp.broadcast_to(
+        owner_ref[...].astype(F32), (2 * ROWS, parcels)
+    ).astype(BF16)
 
     pl.semaphore_wait(barrier, devices - 1)
 
     def send_group(step, unused):
-        first = group_at(step) * ROWS
+        first = (me // batch + devices // batch // 2 + step) % (devices // batch) * batch
         sends = [
-            jnp.where(owner_ref[...] == first + i, vals[...], 0.0).astype(BF16)
-            for i in range(ROWS)
+            jnp.where(
+                owners[...] == (first + i).astype(F32).astype(BF16), vals[...], zero
+            )
+            for i in range(batch)
         ]
         both = lax.dot_general(
             jnp.concatenate(sends, axis=0), hot[...], NT, preferred_element_type=F32
         )
-        for i in range(ROWS):
+        for i in range(batch):
             at = 2 * ROWS * i
             packed[first + i] = both[at : at + ROWS] + both[at + ROWS : at + 2 * ROWS]
 
@@ -161,15 +174,15 @@
 
             return carried
 
-        return lax.fori_loop(0, ROWS, launch, unused)
-
-    lax.fori_loop(0, groups, send_group, 0)
+        return lax.fori_loop(0, batch, launch, unused)
+
+    lax.fori_loop(0, devices // batch, send_group, 0)
     got[me] = packed[me]
 
     fields = jnp.concatenate([dens_ref[...], rest_ref[...].reshape(4 * slab_x, slab_y)], axis=0)
     tab = jnp.concatenate(split(fields), axis=1).astype(BF16)
     total[...] = jnp.zeros_like(total)
-    ys = iota((slab_y, capacity), 0)
+    ys = iota((slab_y, capacity), 0).astype(F32).astype(BF16)
     xs = iota((slab_x, capacity), 0)
 
     def take_group(step, unused):
@@ -192,7 +205,9 @@
 
         for i in range(ROWS):
             cell = cell_of(i)
-            lane_hot = jnp.where(ys == cell % slab_y, 1.0, 0.0).astype(BF16)
+            lane_hot = jnp.where(
+                ys == (cell % slab_y).astype(F32).astype(BF16), one, zero
+            )
             spot[:, i * capacity : (i + 1) * capacity] = lane_hot
             found = jnp.dot(
                 tab, jnp.concatenate([lane_hot, lane_hot], axis=0), preferred_element_type=F32
@@ -310,10 +325,7 @@
             pltpu.roll(here, slab_y - 1, 1),
         )
         smooth = 0.4 * here + 0.15 * (below + above + right + left)
-        if c == 0:
-            new_dens_ref[...] = dens_ref[...] + smooth
-        else:
-            new_rest_ref[c - 1] = rest_ref[c - 1] + smooth
+        smooth_ref[c] = smooth
 
     for out_ref, in_ref, side, base, target, sends, takes in edges:
 
@@ -332,17 +344,15 @@
     capacity = -(-max(2, 4 * parcels // devices) // LANES) * LANES
     vmem = pl.BlockSpec(memory_space=pltpu.VMEM)
     smem = pl.BlockSpec(memory_space=pltpu.SMEM)
-    return pl.pallas_call(
+    smooth = pl.pallas_call(
         functools.partial(fused_kernel, width_x, width_y, capacity),
-        out_shape=(
-            jax.ShapeDtypeStruct(gas_density.shape, F32),
-            jax.ShapeDtypeStruct(gas_rest.shape, F32),
-        ),
+        out_shape=jax.ShapeDtypeStruct((5, slab_x, slab_y), F32),
         in_specs=[vmem] * 5 + [smem] + [vmem] * 2,
-        out_specs=(vmem, vmem),
+        out_specs=vmem,
         scratch_shapes=[
             pltpu.VMEM((capacity, parcels), BF16),
-            pltpu.VMEM((2 * ROWS, parcels), F32),
+            pltpu.VMEM((2 * ROWS, parcels), BF16),
+            pltpu.VMEM((2 * ROWS, parcels), BF16),
             pltpu.VMEM((devices, ROWS, capacity), F32),
             pltpu.VMEM((devices, ROWS, capacity), F32),
             pltpu.VMEM((slab_y, ROWS * capacity), BF16),
@@ -369,6 +379,7 @@
         gas_density,
         gas_rest,
     )
+    return (gas_density + smooth[0], gas_rest + smooth[1:])
 
 
 def solution(mesh):

time: 36 us -> 34.7 us (0.964)
  the two profiles are of different devices: /device:TPU:0 before, /device:TPU:27 now
where the time goes in v2:
time: 34.7 us; the launch traced here: 34.4 us
  Pallas kernels  31 us (89%)
  other arithmetic  2.8 us (8%)
  between operations  0.66 us (2%)
    pallas_call x1, Pallas kernels, per_device(): pl.pallas_call(functools.partial(fused_kernel, width_x, width_y, capacity...  31 us
    add x2, other arithmetic, per_device(): return (gas_density + smooth[0], gas_rest + smooth[1:])  2.8 us

profile of v2, /device:TPU:27, one launch (start us, length us, event | category | flops | bytes accessed | tf_op | source)
XLA Modules:
  0.0 34.4 jit_solution(6313935690390311471)
XLA Ops:
  0.6 0.0 copy-start.1
  0.6 0.0 copy-start
  0.7 31.0 %shard_map.86 = f32[5,32,128]{2,1,0:T(8,128)} custom-call(f32[16,4096]{1,0:T(8,128)} %props_ref.1, s32[1,4096]{1,0:T(1,128)} %bitcast.5, s32[1,4096]{1,0:T(1,128)} %bitcast.6, s32[1,4096]{1,0:T(1,128)} %bitcast.7, f32[8,16]{1,0:T(8,128)} %scalars_ref.1, f32[8,16]{1,0:T(8,128)} %scalars_ref.1, f32[32,128]{1,0:T(8,128)} %dens_ref.1, f32[4,32,128]{2,1,0:T(8,128)} %rest_ref.1), custom_call_target="tpu_custom_call" | custom-call | tf_op jit(solution)/shard_map/pallas_call | solution.py:347
  31.6 0.0 copy-done.1
  31.6 1.3 %bitcast_add_fusion = f32[32,128]{1,0:T(8,128)} fusion(f32[32,128]{1,0:T(8,128)S(1)} %copy-done.1, f32[5,32,128]{2,1,0:T(8,128)} %shard_map.86), kind=kLoop, calls=%fused_computation.1 | loop fusion | flops 4096 | bytes 49152 | tf_op jit(solution)/shard_map/add | solution.py:382
  32.9 0.0 copy-done
  33.0 1.5 %slice_add_fusion = f32[4,32,128]{2,1,0:T(8,128)} fusion(f32[4,32,128]{2,1,0:T(8,128)S(1)} %copy-done, f32[5,32,128]{2,1,0:T(8,128)} %shard_map.86), kind=kLoop, calls=%fused_computation | loop fusion | flops 16384 | bytes 196608 | tf_op jit(solution)/shard_map/add | solution.py:382
Async XLA Ops:
  0.6 31.0 %copy-start.1 = (f32[32,128]{1,0:T(8,128)S(1)}, f32[32,128]{1,0:T(8,128)}, u32[]{:S(2)}) copy-start(f32[32,128]{1,0:T(8,128)} %dens_ref.1) | copy-start | bytes 49156
  0.6 32.3 %copy-start = (f32[4,32,128]{2,1,0:T(8,128)S(1)}, f32[4,32,128]{2,1,0:T(8,128)}, u32[]{:S(2)}) copy-start(f32[4,32,128]{2,1,0:T(8,128)} %rest_ref.1) | copy-start | bytes 196612

commit v3 on v2

--- a/solution.py
+++ b/solution.py
@@ -80,9 +80,15 @@
 
     lax.fori_loop(1, devices, greet, 0)
 
+    pairs = devices // batch
+    plane = me // ROWS
+    inner = (plane + 1) // 2 % 2
+
     def group_at(step):
-        turn = (1 - 2 * (step % 2)) * ((step + 1) // 2)
-        return (me // ROWS + groups // 2 + turn + groups) % groups
+        pair = (plane // 2 + step // 2) % pairs
+        own = (step // 2 == 0).astype(jnp.int32)
+        parity = own * (plane % 2) + (1 - own) * (1 - pair % 2)
+        return 2 * pair + (parity + step) % 2
 
     def copy_to(device):
         return pltpu.make_async_remote_copy(
@@ -151,7 +157,7 @@
     pl.semaphore_wait(barrier, devices - 1)
 
     def send_group(step, unused):
-        first = (me // batch + devices // batch // 2 + step) % (devices // batch) * batch
+        first = (plane // 2 + pairs // 2 * inner + step) % pairs * batch
         sends = [
             jnp.where(
                 owners[...] == (first + i).astype(F32).astype(BF16), vals[...], zero
@@ -166,7 +172,7 @@
             packed[first + i] = both[at : at + ROWS] + both[at + ROWS : at + 2 * ROWS]
 
         def launch(i, carried):
-            device = first + i
+            device = first + (me + i) % batch
 
             @pl.when(device != me)
             def _():
@@ -368,7 +374,7 @@
             pltpu.SemaphoreType.DMA((4,)),
             pltpu.SemaphoreType.DMA((4,)),
         ],
-        compiler_params=pltpu.CompilerParams(collective_id=0, has_side_effects=True),
+        compiler_params=pltpu.CompilerParams(collective_id=0, has_side_effects=True, vmem_limit_bytes=32 * 1024 * 1024),
     )(
         parcel_props,
         size_class.reshape(1, parcels),

time: 34.7 us -> 36.7 us (1.058)
  the two profiles are of different devices: /device:TPU:27 before, /device:TPU:1 now
where the time goes in v3:
time: 36.7 us; the launch traced here: 36.1 us
  Pallas kernels  28.9 us (79%)
  local copies, waits for them, and re-layouts  5.34 us (15%)
  other arithmetic  1.25 us (3%)
  between operations  0.66 us (2%)
    pallas_call x1, Pallas kernels, per_device(): pl.pallas_call(functools.partial(fused_kernel, width_x, width_y, capacity...  28.9 us
    unnamed x14, local copies, waits for them, and re-layouts  5.34 us
    add x2, other arithmetic, per_device(): return (gas_density + smooth[0], gas_rest + smooth[1:])  1.25 us

profile of v3, /device:TPU:1, one launch (start us, length us, event | category | flops | bytes accessed | tf_op | source)
XLA Modules:
  0.0 36.1 jit_solution(5162302149495250645)
XLA Ops:
  0.6 0.0 copy-start.3
  0.6 0.7 %copy-done.3 = f32[8,16]{1,0:T(8,128)S(1)} copy-done((f32[8,16]{1,0:T(8,128)S(1)}, f32[8,16]{1,0:T(8,128)}, u32[]{:S(2)}) %copy-start.3) | copy-done | bytes 536
  1.3 0.0 copy-start
  1.3 0.9 %copy-done = f32[16,4096]{1,0:T(8,128)S(1)} copy-done((f32[16,4096]{1,0:T(8,128)S(1)}, f32[16,4096]{1,0:T(8,128)}, u32[]{:S(2)}) %copy-start) | copy-done | bytes 262168
  2.3 0.0 copy-start.1
  2.3 0.8 %copy-done.1 = f32[4,32,128]{2,1,0:T(8,128)S(1)} copy-done((f32[4,32,128]{2,1,0:T(8,128)S(1)}, f32[4,32,128]{2,1,0:T(8,128)}, u32[]{:S(2)}) %copy-start.1) | copy-done | bytes 65560
  3.1 0.0 copy-start.2
  3.1 0.7 %copy-done.2 = f32[32,128]{1,0:T(8,128)S(1)} copy-done((f32[32,128]{1,0:T(8,128)S(1)}, f32[32,128]{1,0:T(8,128)}, u32[]{:S(2)}) %copy-start.2) | copy-done | bytes 16408
  3.8 0.0 copy-start.4
  3.8 0.7 %copy-done.4 = s32[4096]{0:T(1024)S(1)} copy-done((s32[4096]{0:T(1024)S(1)}, s32[4096]{0:T(1024)}, u32[]{:S(2)}) %copy-start.4) | copy-done | bytes 16408
  4.5 0.0 copy-start.5
  4.5 0.7 %copy-done.5 = s32[4096,1]{0,1:T(1,128)S(1)} copy-done((s32[4096,1]{0,1:T(1,128)S(1)}, s32[4096,1]{0,1:T(1,128)}, u32[]{:S(2)}) %copy-start.5) | copy-done | bytes 16408
  5.3 0.0 copy-start.6
  5.3 0.7 %copy-done.6 = s32[4096]{0:T(1024)S(1)} copy-done((s32[4096]{0:T(1024)S(1)}, s32[4096]{0:T(1024)}, u32[]{:S(2)}) %copy-start.6) | copy-done | bytes 16408
  6.0 28.9 %shard_map.86 = f32[5,32,128]{2,1,0:T(8,128)S(1)} custom-call(f32[16,4096]{1,0:T(8,128)S(1)} %copy-done, s32[1,4096]{1,0:T(1,128)S(1)} %bitcast.5, s32[1,4096]{1,0:T(1,128)S(1)} %bitcast.6, s32[1,4096]{1,0:T(1,128)S(1)} %bitcast.7, f32[8,16]{1,0:T(8,128)S(1)} %copy-done.3, f32[8,16]{1,0:T(8,128)S(1)} %copy-done.3, f32[32,128]{1,0:T(8,128)S(1)} %copy-done.2, ...), custom_call_target="tpu_custom_call" | custom-call | tf_op jit(solution)/shard_map/pallas_call | solution.py:353
  34.9 0.6 %bitcast_add_fusion = f32[32,128]{1,0:T(8,128)} fusion(f32[32,128]{1,0:T(8,128)S(1)} %copy-done.2, f32[5,32,128]{2,1,0:T(8,128)S(1)} %shard_map.86), kind=kLoop, calls=%fused_computation.1 | loop fusion | flops 4096 | bytes 49152 | tf_op jit(solution)/shard_map/add | solution.py:388
  35.5 0.6 %slice_add_fusion = f32[4,32,128]{2,1,0:T(8,128)} fusion(f32[4,32,128]{2,1,0:T(8,128)S(1)} %copy-done.1, f32[5,32,128]{2,1,0:T(8,128)S(1)} %shard_map.86), kind=kLoop, calls=%fused_computation | loop fusion | flops 16384 | bytes 196608 | tf_op jit(solution)/shard_map/add | solution.py:388
Async XLA Ops:
  0.6 0.7 %copy-start.3 = (f32[8,16]{1,0:T(8,128)S(1)}, f32[8,16]{1,0:T(8,128)}, u32[]{:S(2)}) copy-start(f32[8,16]{1,0:T(8,128)} %scalars_ref.1) | copy-start | bytes 1540
  1.3 0.9 %copy-start = (f32[16,4096]{1,0:T(8,128)S(1)}, f32[16,4096]{1,0:T(8,128)}, u32[]{:S(2)}) copy-start(f32[16,4096]{1,0:T(8,128)} %props_ref.1) | copy-start | bytes 786436
  2.3 0.8 %copy-start.1 = (f32[4,32,128]{2,1,0:T(8,128)S(1)}, f32[4,32,128]{2,1,0:T(8,128)}, u32[]{:S(2)}) copy-start(f32[4,32,128]{2,1,0:T(8,128)} %rest_ref.1) | copy-start | bytes 196612
  3.1 0.7 %copy-start.2 = (f32[32,128]{1,0:T(8,128)S(1)}, f32[32,128]{1,0:T(8,128)}, u32[]{:S(2)}) copy-start(f32[32,128]{1,0:T(8,128)} %dens_ref.1) | copy-start | bytes 49156
  3.8 0.7 %copy-start.4 = (s32[4096]{0:T(1024)S(1)}, s32[4096]{0:T(1024)}, u32[]{:S(2)}) copy-start(s32[4096]{0:T(1024)} %param.8) | copy-start | bytes 49156
  4.5 0.7 %copy-start.5 = (s32[4096,1]{0,1:T(1,128)S(1)}, s32[4096,1]{0,1:T(1,128)}, u32[]{:S(2)}) copy-start(s32[4096,1]{0,1:T(1,128)} %param.9) | copy-start | bytes 49156
  5.3 0.7 %copy-start.6 = (s32[4096]{0:T(1024)S(1)}, s32[4096]{0:T(1024)}, u32[]{:S(2)}) copy-start(s32[4096]{0:T(1024)} %param.10) | copy-start | bytes 49156
